TPU v7x, 32 devices: a whole 2x2x4 slice. The times are simulated.
32 devices in a mesh: tiles: 16 (over z, x, core), strip: 2 (over y).
Axes of the slice: x: 2, y: 2, z: 4, core: 2. Of those that a mesh axis runs over, the one named last changes fastest.
Arguments:
- fields: float32 [16, 2, 3, 3, 4, 8100], P('tiles', 'strip'), may hold values from -6 to 6
- wet_land: int32 [16, 2, 3, 8100], P('tiles', 'strip'), may hold values from 0 to 1, as said below
- links: int32 [16, 2, 3, 4, 4], P('tiles', 'strip'), may hold values from -1 to 3, as said below
- surface_diagonal: float32 [16, 2, 3, 8100], P('tiles', 'strip'), may hold values from 0.25 to 2
- spread: float32 [3, 4], replicated, may hold values from 0.02 to 0.2
- mixing: float32 [4], replicated, may hold values from 0.02 to 0.2
- thickness: float32 [4], replicated, may hold values from 0.5 to 2
Outputs:
- adjoint_fields: float32 [16, 2, 3, 3, 4, 8100], P('tiles', 'strip')
- surface_solution: float32 [16, 2, 3, 8100], P('tiles', 'strip')
- surface_residual: float32 [16, 2, 3, 8100], P('tiles', 'strip')
Inputs may be any that keep to these rules, and one draw needn't show every extreme that they name: wet_land is 1 on most cells of the first 1 to 3 slots of each device and 0 on all cells of its other slots. Offsets dt and ds are -1, 0 or 1; on the west and east sides dt is -1 and 1, on the south and north sides ds is -1 and 1; a partner slot is -1 or a slot that holds wet cells; links are mutual: side e of slot k pairs with side e XOR 1 of its partner, whose entry points back with opposite offsets and rotation code (4 - code) mod 4; an empty slot has no links; rotation codes are 0 to 3.
All inputs are finite; a program needn't handle non-finite values.
Results may differ from a plain program's by a relative error of at most 0.00027.
Values sent between devices are 32-bit elements; how exact they have to be, the bound alone decides.
A program may use at most 64 MiB of HBM per device.

v0:
```python
import jax
import jax.numpy as jnp
import numpy as np
from jax import lax
from jax.sharding import PartitionSpec as P

TILE = 90
SLOTS = 3
ITERS = 2


OPPOSITE = np.array([1, 0, 3, 2], np.int32)


def extended(value, sides, width):
    for axis, dim in sides:
        peers, length = (lax.axis_size(axis), value.shape[dim])
        up = [(i, (i + 1) % peers) for i in range(peers)]
        down = [(j, i) for i, j in up]
        last = lax.slice_in_dim(value, length - width, length, axis=dim)
        leading = lax.slice_in_dim(value, 0, width, axis=dim)
        before = lax.ppermute(last, axis, up)
        after = lax.ppermute(leading, axis, down)
        value = jnp.concatenate([before, value, after], axis=dim)
    return value


def rim_rows(values, width):
    west_rim = values[..., ::width]
    east_rim = values[..., width - 1 :: width]
    south_rim = values[..., :width]
    north_rim = values[..., -width:]
    return jnp.concatenate([west_rim, east_rim, south_rim, north_rim], axis=-1)


def beside_values(values, rims, width):
    cells_total = values.shape[-1]
    leading = values.shape[:-1]
    places = jnp.arange(cells_total, dtype=jnp.int32)
    column_index = places % width
    row_index = places // width
    west_full = jnp.broadcast_to(rims[..., 0, :, None], leading + (width, width)).reshape(
        leading + (cells_total,)
    )
    east_full = jnp.broadcast_to(rims[..., 1, :, None], leading + (width, width)).reshape(
        leading + (cells_total,)
    )
    south_full = jnp.broadcast_to(rims[..., 2, None, :], leading + (width, width)).reshape(
        leading + (cells_total,)
    )
    north_full = jnp.broadcast_to(rims[..., 3, None, :], leading + (width, width)).reshape(
        leading + (cells_total,)
    )
    zero_cell = jnp.zeros(leading + (1,), jnp.float32)
    zero_line = jnp.zeros(leading + (width,), jnp.float32)
    west_side = jnp.where(
        column_index == 0, west_full, jnp.concatenate([zero_cell, values[..., :-1]], -1)
    )
    east_side = jnp.where(
        column_index == width - 1, east_full, jnp.concatenate([values[..., 1:], zero_cell], -1)
    )
    south_side = jnp.where(
        row_index == 0, south_full, jnp.concatenate([zero_line, values[..., :-width]], -1)
    )
    north_side = jnp.where(
        row_index == width - 1, north_full, jnp.concatenate([values[..., width:], zero_line], -1)
    )
    return (west_side, east_side, south_side, north_side)


def orient(picked, links, vector):
    code = links[..., 3]
    partner = links[..., 2]
    lead = code.ndim
    extra = picked.ndim - lead
    tail_shape = code.shape + (1,) * extra
    flipped = jnp.where((code != 0).reshape(tail_shape), jnp.flip(picked, -1), picked)
    flipped = flipped * (partner >= 0).astype(jnp.float32).reshape(tail_shape)
    if vector:
        turn_shape = code.shape + (1,) * (extra - 1)
        cosine_part = ((code == 0).astype(jnp.float32) - (code == 2).astype(jnp.float32)).reshape(
            turn_shape
        )
        sine_part = ((code == 1).astype(jnp.float32) - (code == 3).astype(jnp.float32)).reshape(
            turn_shape
        )
        eastward = jnp.take(flipped, 0, axis=lead)
        northward = jnp.take(flipped, 1, axis=lead)
        scalar_part = jnp.take(flipped, 2, axis=lead)
        flipped = jnp.stack(
            [
                cosine_part * eastward + sine_part * northward,
                cosine_part * northward - sine_part * eastward,
                scalar_part,
            ],
            axis=lead,
        )
    return jnp.moveaxis(flipped, lead - 1, -2)


def slab_step(fields, wet, rims, spread, mixing, thickness, width):
    wet_cells = wet[..., None, None, :]
    masked = fields * wet_cells
    west_side, east_side, south_side, north_side = beside_values(masked, rims, width)
    flat_term = west_side + east_side + south_side + north_side - 4.0 * masked
    above = jnp.concatenate([masked[..., 1:, :], masked[..., -1:, :]], axis=-2)
    below = jnp.concatenate([masked[..., :1, :], masked[..., :-1, :]], axis=-2)
    column_term = above + below - 2.0 * masked
    updated = wet_cells * (masked + spread[:, :, None] * flat_term + mixing[:, None] * column_term)
    flux = 0.5 * (
        east_side[..., 0, :, :]
        - west_side[..., 0, :, :]
        + north_side[..., 1, :, :]
        - south_side[..., 1, :, :]
    )
    source = wet * jnp.sum(thickness[:, None] * flux, axis=-2)
    return (updated, source)


def surface_apply(values, wet, rims, diagonal, width):
    west_side, east_side, south_side, north_side = beside_values(values, rims, width)
    return wet * ((4.0 + diagonal) * values - (west_side + east_side + south_side + north_side))


def pick_local(tile_packs, flat_index):
    opposite = jnp.broadcast_to(jnp.asarray(OPPOSITE)[None, :], flat_index.shape)
    return tile_packs[flat_index, ..., opposite, :]


def paired_totals(residual, image):
    return lax.psum((jnp.sum(residual * residual), jnp.sum(residual * image)), ("tiles", "strip"))


def on_device(fields, wet_land, links, surface_diagonal, spread, mixing, thickness):
    local_fields = fields[0, 0]
    wet = wet_land[0, 0].astype(jnp.float32)
    local_links = links[0, 0]
    diagonal = surface_diagonal[0, 0]
    group_shift = local_links[..., 0]
    strip_shift = local_links[..., 1]
    partner = jnp.maximum(local_links[..., 2], 0)
    near_index = ((group_shift + 1) * 3 + strip_shift + 1) * SLOTS + partner
    masked = local_fields * wet[:, None, None, :]
    slab_pack = rim_rows(masked, TILE)[None, None]
    neighbours = extended(slab_pack, (("tiles", 0), ("strip", 1)), 1)
    slab_packs = neighbours.reshape((-1,) + masked.shape[1:-1] + (4, TILE))
    picked = pick_local(slab_packs, near_index)
    slab_rims = orient(picked, local_links, True)
    updated, source = slab_step(local_fields, wet, slab_rims, spread, mixing, thickness, TILE)

    def surface_image(values):
        surface_pack = rim_rows(values, TILE)[None, None]
        surface_near = extended(surface_pack, (("tiles", 0), ("strip", 1)), 1)
        surface_packs = surface_near.reshape((-1, 4, TILE))
        rims = orient(pick_local(surface_packs, near_index), local_links, False)
        return surface_apply(values, wet, rims, diagonal, TILE)

    solution = jnp.zeros_like(source)
    residual = source
    image = surface_image(residual)
    norm_now, product = paired_totals(residual, image)
    alpha = norm_now / product
    direction = residual
    conjugate = image
    for iteration in range(ITERS):
        solution = solution + alpha * direction
        residual = residual - alpha * conjugate
        if iteration + 1 < ITERS:
            image = surface_image(residual)
            norm_next, product = paired_totals(residual, image)
            ratio = norm_next / norm_now
            alpha = norm_next / (product - ratio * norm_next / alpha)
            direction = residual + ratio * direction
            conjugate = image + ratio * conjugate
            norm_now = norm_next
    return (updated[None, None], solution[None, None], residual[None, None])


def solution(mesh):
    placed = (
        P("tiles", "strip", None, None, None, None),
        P("tiles", "strip", None, None),
        P("tiles", "strip", None, None, None),
        P("tiles", "strip", None, None),
        P(),
        P(),
        P(),
    )
    return jax.shard_map(
        on_device,
        mesh=mesh,
        in_specs=placed,
        out_specs=(
            P("tiles", "strip", None, None, None, None),
            P("tiles", "strip", None, None),
            P("tiles", "strip", None, None),
        ),
        check_vma=False,
    )
```

profile of v0, /device:TPU:0, one launch (start us, length us, event | category | flops | bytes accessed | tf_op | source)
XLA Modules:
  0.0 161.9 jit_solution(17150465389011027708)
XLA Ops:
  0.6 1.0 fusion.12
  1.6 1.5 bitcast_multiply_fusion
  3.2 1.0 slice.150
  4.2 1.0 slice.151
  5.3 0.5 collective-permute-start
  5.8 5.0 %collective-permute-start.1 = (f32[1,1,3,3,4,360]{5,4,3,2,1,0:T(4,128)S(1)}, f32[1,1,3,3,4,360]{5,4,3,2,1,0:T(4,128)S(1)}, u32[]{:S(2)}, u32[]{:S(2)}) collective-permute-start(f32[1,1,3,3,4,360]{5,4,3,2,1,0:T(4,128)S(1)} %maximum_bitcast_fusion.1), channel_id=1, source_target_pairs={{2,0},{4,2},{6,4},{8,6},{10,8},{12,10},{14,12},{16,14},{18,16},{20... | collective-permute-start | bytes 155528 | tf_op jit(solution)/shard_map/ppermute | solution.py:23
  10.9 2.1 %fusion.32 = (f32[3,3,4,8099]{3,2,1,0:T(4,128)}, f32[3,3,4,8099]{3,2,1,0:T(4,128)}) fusion(f32[3,3,4,8100]{3,2,1,0:T(4,128)S(1)} %bitcast_multiply_fusion), kind=kLoop, calls=%fused_computation.98 | loop fusion | bytes 4665024 | tf_op jit(solution)/shard_map/slice | solution.py:57
  13.0 2.0 %fusion.35 = (f32[3,3,3,8100]{3,2,1,0:T(4,128)}, f32[3,3,3,8100]{3,2,1,0:T(4,128)}) fusion(f32[3,3,4,8100]{3,2,1,0:T(4,128)S(1)} %bitcast_multiply_fusion), kind=kLoop, calls=%fused_computation.101 | loop fusion | bytes 3499200 | tf_op jit(solution)/shard_map/slice | solution.py:107
  15.0 2.1 %fusion.31 = (f32[3,3,4,8010]{3,2,1,0:T(4,128)}, f32[3,3,4,8010]{3,2,1,0:T(4,128)}) fusion(f32[3,3,4,8100]{3,2,1,0:T(4,128)S(1)} %bitcast_multiply_fusion), kind=kLoop, calls=%fused_computation.97 | loop fusion | bytes 4613760 | tf_op jit(solution)/shard_map/slice | solution.py:66
  17.1 1.3 fusion.34
  18.5 0.2 fusion.27
  18.8 2.0 %collective-permute-start.2 = (f32[3,1,3,3,4,360]{5,4,3,2,1,0:T(4,128)S(1)}, f32[3,1,3,3,4,360]{5,4,3,2,1,0:T(4,128)S(1)}, u32[]{:S(2)}, u32[]{:S(2)}) collective-permute-start(f32[3,1,3,3,4,360]{5,4,3,2,1,0:T(4,128)S(1)} %pad_maximum_fusion.1), channel_id=1, source_target_pairs={{0,1},{1,0},{2,3},{3,2},{4,5},{5,4},{6,7},{7,6},{8,9},{9,8},{10,11... | collective-permute-start | bytes 466568 | tf_op jit(solution)/shard_map/ppermute | solution.py:22
  20.9 0.2 compare_reduce_fusion
  21.4 3.0 %collective-permute-done.2 = f32[3,1,3,3,4,360]{5,4,3,2,1,0:T(4,128)S(1)} collective-permute-done((f32[3,1,3,3,4,360]{5,4,3,2,1,0:T(4,128)S(1)}, f32[3,1,3,3,4,360]{5,4,3,2,1,0:T(4,128)S(1)}, u32[]{:S(2)}, u32[]{:S(2)}) %collective-permute-start.2) | collective-permute-done | bytes 155552 | tf_op jit(solution)/shard_map/ppermute | solution.py:22
  24.4 1.8 %collective-permute-done.3 = f32[3,1,3,3,4,360]{5,4,3,2,1,0:T(4,128)S(1)} collective-permute-done((f32[3,1,3,3,4,360]{5,4,3,2,1,0:T(4,128)S(1)}, f32[3,1,3,3,4,360]{5,4,3,2,1,0:T(4,128)S(1)}, u32[]{:S(2)}, u32[]{:S(2)}) %collective-permute-start.3) | collective-permute-done | bytes 155552 | tf_op jit(solution)/shard_map/ppermute | solution.py:23
  26.3 0.5 reshape.189
  26.9 0.7 gather_fusion
  28.1 0.5 broadcast_in_dim.203
  28.6 2.6 %reshape.190 = f32[3,3,4,8100]{3,2,1,0:T(4,128)} reshape(f32[3,3,4,90,90]{4,3,2,1,0:T(8,128)S(1)} %broadcast_in_dim.203) | data formatting | bytes 2332800 | tf_op jit(solution)/shard_map/reshape | solution.py:42
  31.2 0.5 broadcast_in_dim.206
  31.7 2.5 %reshape.191 = f32[3,3,4,8100]{3,2,1,0:T(4,128)} reshape(f32[3,3,4,90,90]{4,3,2,1,0:T(8,128)S(1)} %broadcast_in_dim.206) | data formatting | bytes 2332800 | tf_op jit(solution)/shard_map/reshape | solution.py:45
  34.3 2.5 %reshape.192 = f32[3,3,4,8100]{3,2,1,0:T(4,128)} reshape(f32[3,3,4,90,90]{4,3,2,1,0:T(8,128)S(1)} %broadcast_in_dim.209) | data formatting | bytes 2332800 | tf_op jit(solution)/shard_map/reshape | solution.py:48
  37.0 2.5 %reshape.193 = f32[3,3,4,8100]{3,2,1,0:T(4,128)} reshape(f32[3,3,4,90,90]{4,3,2,1,0:T(8,128)S(1)} %broadcast_in_dim.212) | data formatting | bytes 2332800 | tf_op jit(solution)/shard_map/reshape | solution.py:51
  39.6 7.3 %fusion.4 = (f32[1,1,3,3,4,8100]{5,4,3,2,1,0:T(4,128)}, f32[3,3,4,8100]{3,2,1,0:T(4,128)S(1)}, f32[3,3,4,8100]{3,2,1,0:T(4,128)S(1)}, f32[3,3,4,8100]{3,2,1,0:T(4,128)S(1)}, f32[3,3,4,8100]{3,2,1,0:T(4,128)S(1)}) fusion(f32[3,3,1,8100]{3,2,1,0:T(1,128)} %get-tuple-element.64, f32[3,3,3,8100]{3,2,1,0:T(4,128)} %get-tuple-element.66, ...), kind=kLoop, calls=%fused_computation.8 | loop fusion | flops 5832000 | bytes 18765856 | tf_op jit(solution)/shard_map/broadcast_in_dim | solution.py:176
  46.8 0.5 fusion.7
  47.3 0.4 copy-done.1
  48.1 0.2 slice.174
  48.4 4.4 %collective-permute-start.5 = (f32[1,1,3,360]{3,2,1,0:T(4,128)S(1)}, f32[1,1,3,360]{3,2,1,0:T(4,128)S(1)}, u32[]{:S(2)}, u32[]{:S(2)}) collective-permute-start(f32[1,1,3,360]{3,2,1,0:T(4,128)S(1)} %maximum_bitcast_fusion.2), channel_id=1, source_target_pairs={{2,0},{4,2},{6,4},{8,6},{10,8},{12,10},{14,12},{16,14},{18,16},{20... | collective-permute-start | bytes 12968 | tf_op jit(solution)/shard_map/ppermute | solution.py:23
  52.9 1.2 collective-permute-done.4
  54.2 1.8 %collective-permute-start.6 = (f32[3,1,3,360]{3,2,1,0:T(4,128)S(1)}, f32[3,1,3,360]{3,2,1,0:T(4,128)S(1)}, u32[]{:S(2)}, u32[]{:S(2)}) collective-permute-start(f32[3,1,3,360]{3,2,1,0:T(4,128)S(1)} %pad_maximum_fusion.4), channel_id=1, source_target_pairs={{0,1},{1,0},{2,3},{3,2},{4,5},{5,4},{6,7},{7,6},{8,9},{9,8},{10,11... | collective-permute-start | bytes 38888 | tf_op jit(solution)/shard_map/ppermute | solution.py:22
  56.0 0.3 collective-permute-start.7
  56.4 1.6 collective-permute-done.6
  58.0 1.8 %collective-permute-done.7 = f32[3,1,3,360]{3,2,1,0:T(4,128)S(1)} collective-permute-done((f32[3,1,3,360]{3,2,1,0:T(4,128)S(1)}, f32[3,1,3,360]{3,2,1,0:T(4,128)S(1)}, u32[]{:S(2)}, u32[]{:S(2)}) %collective-permute-start.7) | collective-permute-done | bytes 12992 | tf_op jit(solution)/shard_map/ppermute | solution.py:23
  59.9 0.7 gather_fusion.1
  60.9 0.2 reshape.195
  61.8 1.0 multiply_reduce_fusion.2
  62.7 37.6 %all-reduce.13 = (f32[]{:T(128)}, f32[]{:T(128)}) all-reduce(f32[]{:T(128)} %get-tuple-element.42, f32[]{:T(128)} %get-tuple-element.41), channel_id=1, replica_groups=mesh['tiles'=16,'strip'=2] {'tiles','strip'}, use_global_device_ids=true, to_apply=%region_2.6 | all-reduce | flops 2 | bytes 16 | tf_op jit(solution)/shard_map/psum | solution.py:131
  102.0 0.2 slice.186
  102.3 4.4 %collective-permute-start.9 = (f32[1,1,3,360]{3,2,1,0:T(4,128)S(1)}, f32[1,1,3,360]{3,2,1,0:T(4,128)S(1)}, u32[]{:S(2)}, u32[]{:S(2)}) collective-permute-start(f32[1,1,3,360]{3,2,1,0:T(4,128)S(1)} %maximum_bitcast_fusion.3), channel_id=1, source_target_pairs={{2,0},{4,2},{6,4},{8,6},{10,8},{12,10},{14,12},{16,14},{18,16},{20... | collective-permute-start | bytes 12968 | tf_op jit(solution)/shard_map/ppermute | solution.py:23
  106.9 1.2 collective-permute-done.8
  108.1 2.5 %collective-permute-start.10 = (f32[3,1,3,360]{3,2,1,0:T(4,128)S(1)}, f32[3,1,3,360]{3,2,1,0:T(4,128)S(1)}, u32[]{:S(2)}, u32[]{:S(2)}) collective-permute-start(f32[3,1,3,360]{3,2,1,0:T(4,128)S(1)} %pad_maximum_fusion.5), channel_id=1, source_target_pairs={{0,1},{1,0},{2,3},{3,2},{4,5},{5,4},{6,7},{7,6},{8,9},{9,8},{10,11... | collective-permute-start | bytes 38888 | tf_op jit(solution)/shard_map/ppermute | solution.py:22
  110.8 1.5 collective-permute-done.10
  112.3 2.0 %collective-permute-done.11 = f32[3,1,3,360]{3,2,1,0:T(4,128)S(1)} collective-permute-done((f32[3,1,3,360]{3,2,1,0:T(4,128)S(1)}, f32[3,1,3,360]{3,2,1,0:T(4,128)S(1)}, u32[]{:S(2)}, u32[]{:S(2)}) %collective-permute-start.11) | collective-permute-done | bytes 12992 | tf_op jit(solution)/shard_map/ppermute | solution.py:23
  114.5 0.7 gather_fusion.2
  116.4 1.0 multiply_reduce_fusion
  117.4 38.4 %all-reduce.12 = (f32[]{:T(128)}, f32[]{:T(128)}) all-reduce(f32[]{:T(128)} %get-tuple-element.40, f32[]{:T(128)} %get-tuple-element.39), channel_id=1, replica_groups=mesh['tiles'=16,'strip'=2] {'tiles','strip'}, use_global_device_ids=true, to_apply=%region_6.10 | all-reduce | flops 2 | bytes 16 | tf_op jit(solution)/shard_map/psum | solution.py:131
  160.5 0.7 broadcast_in_dim.237
  161.2 0.7 broadcast_in_dim.238
  (95 shorter events, 5.5 us)
Async XLA Ops:
  5.3 13.5 %collective-permute-start = (f32[1,1,3,3,4,360]{5,4,3,2,1,0:T(4,128)S(1)}, f32[1,1,3,3,4,360]{5,4,3,2,1,0:T(4,128)S(1)}, u32[]{:S(2)}, u32[]{:S(2)}) collective-permute-start(f32[1,1,3,3,4,360]{5,4,3,2,1,0:T(4,128)S(1)} %maximum_bitcast_fusion.1), channel_id=1, source_target_pairs={{0,2},{2,4},{4,6},{6,8},{8,10},{10,12},{12,14},{14,16},{16,18},{18... | collective-permute-start | bytes 155528 | tf_op jit(solution)/shard_map/ppermute | solution.py:22
  5.8 12.9 %collective-permute-start.1 = (f32[1,1,3,3,4,360]{5,4,3,2,1,0:T(4,128)S(1)}, f32[1,1,3,3,4,360]{5,4,3,2,1,0:T(4,128)S(1)}, u32[]{:S(2)}, u32[]{:S(2)}) collective-permute-start(f32[1,1,3,3,4,360]{5,4,3,2,1,0:T(4,128)S(1)} %maximum_bitcast_fusion.1), channel_id=1, source_target_pairs={{2,0},{4,2},{6,4},{8,6},{10,8},{12,10},{14,12},{16,14},{18,16},{20... | collective-permute-start | bytes 155528 | tf_op jit(solution)/shard_map/ppermute | solution.py:23
  17.1 1.4 copy-start.7
  17.1 1.4 copy-start.3
  17.1 1.4 copy-start.6
  18.8 5.6 %collective-permute-start.2 = (f32[3,1,3,3,4,360]{5,4,3,2,1,0:T(4,128)S(1)}, f32[3,1,3,3,4,360]{5,4,3,2,1,0:T(4,128)S(1)}, u32[]{:S(2)}, u32[]{:S(2)}) collective-permute-start(f32[3,1,3,3,4,360]{5,4,3,2,1,0:T(4,128)S(1)} %pad_maximum_fusion.1), channel_id=1, source_target_pairs={{0,1},{1,0},{2,3},{3,2},{4,5},{5,4},{6,7},{7,6},{8,9},{9,8},{10,11... | collective-permute-start | bytes 466568 | tf_op jit(solution)/shard_map/ppermute | solution.py:22
  20.8 5.3 %collective-permute-start.3 = (f32[3,1,3,3,4,360]{5,4,3,2,1,0:T(4,128)S(1)}, f32[3,1,3,3,4,360]{5,4,3,2,1,0:T(4,128)S(1)}, u32[]{:S(2)}, u32[]{:S(2)}) collective-permute-start(f32[3,1,3,3,4,360]{5,4,3,2,1,0:T(4,128)S(1)} %pad_maximum_fusion.1), channel_id=1, source_target_pairs={{1,0},{0,1},{3,2},{2,3},{5,4},{4,5},{7,6},{6,7},{9,8},{8,9},{11,10... | collective-permute-start | bytes 466568 | tf_op jit(solution)/shard_map/ppermute | solution.py:23
  37.0 2.6 %copy-start = (f32[1,1,3,3,4,8100]{5,4,3,2,1,0:T(4,128)S(1)}, f32[1,1,3,3,4,8100]{5,4,3,2,1,0:T(4,128)}, u32[]{:S(2)}) copy-start(f32[1,1,3,3,4,8100]{5,4,3,2,1,0:T(4,128)} %param.14) | copy-start | bytes 3499204
  37.0 2.6 %copy-start.4 = (f32[3,4]{1,0:T(4,128)S(1)}, f32[3,4]{1,0:T(4,128)}, u32[]{:S(2)}) copy-start(f32[3,4]{1,0:T(4,128)} %param.18) | copy-start | bytes 148
  37.0 2.6 %copy-start.5 = (f32[4]{0:T(128)S(1)}, f32[4]{0:T(128)}, u32[]{:S(2)}) copy-start(f32[4]{0:T(128)} %param.19) | copy-start | bytes 52
  46.8 0.9 copy-start.1
  48.3 5.8 %collective-permute-start.4 = (f32[1,1,3,360]{3,2,1,0:T(4,128)S(1)}, f32[1,1,3,360]{3,2,1,0:T(4,128)S(1)}, u32[]{:S(2)}, u32[]{:S(2)}) collective-permute-start(f32[1,1,3,360]{3,2,1,0:T(4,128)S(1)} %maximum_bitcast_fusion.2), channel_id=1, source_target_pairs={{0,2},{2,4},{4,6},{6,8},{8,10},{10,12},{12,14},{14,16},{16,18},{18... | collective-permute-start | bytes 12968 | tf_op jit(solution)/shard_map/ppermute | solution.py:22
  48.4 5.8 %collective-permute-start.5 = (f32[1,1,3,360]{3,2,1,0:T(4,128)S(1)}, f32[1,1,3,360]{3,2,1,0:T(4,128)S(1)}, u32[]{:S(2)}, u32[]{:S(2)}) collective-permute-start(f32[1,1,3,360]{3,2,1,0:T(4,128)S(1)} %maximum_bitcast_fusion.2), channel_id=1, source_target_pairs={{2,0},{4,2},{6,4},{8,6},{10,8},{12,10},{14,12},{16,14},{18,16},{20... | collective-permute-start | bytes 12968 | tf_op jit(solution)/shard_map/ppermute | solution.py:23
  54.2 7.6 %copy-start.2 = (f32[1,1,3,8100]{3,1,2,0:T(1,128)S(1)}, f32[1,1,3,8100]{3,1,2,0:T(1,128)}, u32[]{:S(2)}) copy-start(f32[1,1,3,8100]{3,1,2,0:T(1,128)} %param.17) | copy-start | bytes 291604
  54.2 3.8 %collective-permute-start.6 = (f32[3,1,3,360]{3,2,1,0:T(4,128)S(1)}, f32[3,1,3,360]{3,2,1,0:T(4,128)S(1)}, u32[]{:S(2)}, u32[]{:S(2)}) collective-permute-start(f32[3,1,3,360]{3,2,1,0:T(4,128)S(1)} %pad_maximum_fusion.4), channel_id=1, source_target_pairs={{0,1},{1,0},{2,3},{3,2},{4,5},{5,4},{6,7},{7,6},{8,9},{9,8},{10,11... | collective-permute-start | bytes 38888 | tf_op jit(solution)/shard_map/ppermute | solution.py:22
  56.0 3.8 %collective-permute-start.7 = (f32[3,1,3,360]{3,2,1,0:T(4,128)S(1)}, f32[3,1,3,360]{3,2,1,0:T(4,128)S(1)}, u32[]{:S(2)}, u32[]{:S(2)}) collective-permute-start(f32[3,1,3,360]{3,2,1,0:T(4,128)S(1)} %pad_maximum_fusion.4), channel_id=1, source_target_pairs={{1,0},{0,1},{3,2},{2,3},{5,4},{4,5},{7,6},{6,7},{9,8},{8,9},{11,10... | collective-permute-start | bytes 38888 | tf_op jit(solution)/shard_map/ppermute | solution.py:23
  102.3 5.8 %collective-permute-start.8 = (f32[1,1,3,360]{3,2,1,0:T(4,128)S(1)}, f32[1,1,3,360]{3,2,1,0:T(4,128)S(1)}, u32[]{:S(2)}, u32[]{:S(2)}) collective-permute-start(f32[1,1,3,360]{3,2,1,0:T(4,128)S(1)} %maximum_bitcast_fusion.3), channel_id=1, source_target_pairs={{0,2},{2,4},{4,6},{6,8},{8,10},{10,12},{12,14},{14,16},{16,18},{18... | collective-permute-start | bytes 12968 | tf_op jit(solution)/shard_map/ppermute | solution.py:22
  102.3 5.8 %collective-permute-start.9 = (f32[1,1,3,360]{3,2,1,0:T(4,128)S(1)}, f32[1,1,3,360]{3,2,1,0:T(4,128)S(1)}, u32[]{:S(2)}, u32[]{:S(2)}) collective-permute-start(f32[1,1,3,360]{3,2,1,0:T(4,128)S(1)} %maximum_bitcast_fusion.3), channel_id=1, source_target_pairs={{2,0},{4,2},{6,4},{8,6},{10,8},{12,10},{14,12},{16,14},{18,16},{20... | collective-permute-start | bytes 12968 | tf_op jit(solution)/shard_map/ppermute | solution.py:23
  108.1 4.2 %collective-permute-start.10 = (f32[3,1,3,360]{3,2,1,0:T(4,128)S(1)}, f32[3,1,3,360]{3,2,1,0:T(4,128)S(1)}, u32[]{:S(2)}, u32[]{:S(2)}) collective-permute-start(f32[3,1,3,360]{3,2,1,0:T(4,128)S(1)} %pad_maximum_fusion.5), channel_id=1, source_target_pairs={{0,1},{1,0},{2,3},{3,2},{4,5},{5,4},{6,7},{7,6},{8,9},{9,8},{10,11... | collective-permute-start | bytes 38888 | tf_op jit(solution)/shard_map/ppermute | solution.py:22
  110.6 3.8 %collective-permute-start.11 = (f32[3,1,3,360]{3,2,1,0:T(4,128)S(1)}, f32[3,1,3,360]{3,2,1,0:T(4,128)S(1)}, u32[]{:S(2)}, u32[]{:S(2)}) collective-permute-start(f32[3,1,3,360]{3,2,1,0:T(4,128)S(1)} %pad_maximum_fusion.5), channel_id=1, source_target_pairs={{1,0},{0,1},{3,2},{2,3},{5,4},{4,5},{7,6},{6,7},{9,8},{8,9},{11,10... | collective-permute-start | bytes 38888 | tf_op jit(solution)/shard_map/ppermute | solution.py:23
where the time goes:
time: 162 us
  blocking collectives  76 us (47%)
  local copies, waits for them, and re-layouts  29.6 us (18%)
  starting transfers between devices  21.2 us (13%)
  waiting for transfers between devices  14.1 us (9%)
  other arithmetic  13.9 us (9%)
  between operations  7.01 us (4%)
    psum x2, blocking collectives, paired_totals(): lax.psum((jnp.sum(residual * residual), jnp.sum(residual * image)), ('til...  76 us
    ppermute x6, starting transfers between devices, extended(): after = lax.ppermute(leading, axis, down)  14.3 us
    ppermute x6, waiting for transfers between devices, extended(): before = lax.ppermute(last, axis, up)  8.48 us
    broadcast_in_dim x1, other arithmetic, on_device(): return (updated[None, None], solution[None, None], residual[None, None])  7.25 us
    ppermute x6, starting transfers between devices, extended(): before = lax.ppermute(last, axis, up)  6.88 us
    ppermute x6, waiting for transfers between devices, extended(): after = lax.ppermute(leading, axis, down)  5.65 us
    slice x2, local copies, waits for them, and re-layouts, slab_step(): below = jnp.concatenate([masked[..., :1, :], masked[..., :-1, :]], axis=-2)  3.3 us
  transfers between devices with their start and end apart: 12, of which 8 were waited for; matrix products, arithmetic and copies ran while one was open for 5% of the time, Pallas kernels for 0%

commit v1 on v0

v1 whole, which is shorter than its diff:
```python
import math

import jax
import jax.numpy as jnp
from jax import lax
from jax.experimental import pallas as pl
from jax.experimental.pallas import tpu as pltpu
from jax.sharding import PartitionSpec as P

LANES = 128
CHUNK = 1024
POS = (0, 3, 1, 2)
GROUP = 16


def offsets(size):
    return (-1, 0, 1) if size >= 3 else tuple(range(size))


def place(offset, size):
    if size >= 3:
        return offset + 1
    return offset * offset if size == 2 else 0 * offset


def roll(value, shift, axis=1):
    size = value.shape[axis]
    shift = shift % size
    return pltpu.roll(value, shift, axis) if shift else value


def build(tiles, strips, slots, fields_n, levels, cells):
    width = math.isqrt(cells)
    n_tiles = -(-cells // CHUNK) * CHUNK // LANES
    wide = n_tiles * LANES
    padded = wide + 2 * LANES
    chunks = wide // CHUNK
    steps_t, steps_s = offsets(tiles), offsets(strips)
    n_s = len(steps_s)
    n_dirs = len(steps_t) * n_s
    low = min(GROUP, tiles)
    high = tiles // low
    first = low * strips
    directions = []
    for dt in steps_t:
        for ds in steps_s:
            if dt == 0 and ds == 0:
                continue
            sides = []
            if dt == -1 or (tiles == 2 and dt):
                sides.append(0)
            if ds == -1 or (strips == 2 and ds):
                sides.append(1)
            if ds == 1:
                sides.append(2)
            if dt == 1:
                sides.append(3)
            here = place(dt, tiles) * n_s + place(ds, strips)
            back = place(-dt if tiles >= 3 else dt, tiles) * n_s + place(-ds if strips >= 3 else ds, strips)
            directions.append((dt, ds, here, back, min(sides), max(sides) + 1))

    def kernel(
        fields, wet_in, links, diag_in, spread, mixing, thick, out_f, out_x, out_r,
        fbuf, wbuf, dbuf, m_ref, w_ref, d_ref, nw_ref, ne_ref, uv_ref, s_ref, u_ref, v_ref, eb_ref, ebs_ref,
        rim_ref, rims_ref, pack1, near1, packb, nearb, pack2, near2, pack3, near3, row_ref, red_ref, red2_ref,
        in_sem, out_sem, send1, recv1, sendb, recvb, send2, recv2, send3, recv3, sendr, recvr, sendq, recvq,
    ):
        t = lax.axis_index("tiles")
        s = lax.axis_index("strip")
        copies = [
            pltpu.make_async_copy(wet_in.at[0, 0], wbuf, in_sem.at[0]),
            pltpu.make_async_copy(diag_in.at[0, 0], dbuf, in_sem.at[1]),
        ] + [pltpu.make_async_copy(fields.at[0, 0, k], fbuf.at[k], in_sem.at[2 + k]) for k in range(slots)]
        for copy in copies:
            copy.start()

        barrier = pltpu.get_barrier_semaphore()
        base = (t // low) * low
        place_t = t % low
        me_first = place_t * strips + s
        peers = 0
        for j in range(1, first):
            other = lax.rem(me_first + j, first)
            pl.semaphore_signal(
                barrier, inc=1, device_id=(base + other // strips, other % strips),
                device_id_type=pl.DeviceIdType.MESH,
            )
            peers += 1
        for j in range(1, high):
            other = lax.rem(t // low + j, high)
            pl.semaphore_signal(
                barrier, inc=1, device_id=(other * low + place_t, s), device_id_type=pl.DeviceIdType.MESH
            )
            peers += 1
        if high > 1:
            for dt, ds, here, back, lo, hi in directions:
                pl.semaphore_signal(
                    barrier, inc=1,
                    device_id=(lax.rem(t + dt + tiles, tiles), lax.rem(s + ds + strips, strips)),
                    device_id_type=pl.DeviceIdType.MESH,
                )
                peers += 1

        def exchange(pack, near, send_sem, recv_sem):
            out = []
            for dt, ds, here, back, lo, hi in directions:
                copy = pltpu.make_async_remote_copy(
                    src_ref=pack.at[pl.ds(lo, hi - lo)],
                    dst_ref=near.at[back, pl.ds(lo, hi - lo)],
                    send_sem=send_sem.at[here],
                    recv_sem=recv_sem.at[back],
                    device_id=(lax.rem(t + dt + tiles, tiles), lax.rem(s + ds + strips, strips)),
                    device_id_type=pl.DeviceIdType.MESH,
                )
                copy.start()
                out.append(copy)
            return out

        lane = lax.broadcasted_iota(jnp.int32, (1, LANES), 1)
        flip_at = jnp.where(lane < width, width - 1 - lane, lane)

        def flip(value):
            rows = value.shape[0]
            if rows < 8:
                value = jnp.concatenate([value, jnp.zeros((8 - rows, LANES), jnp.float32)], 0)
            at = jnp.broadcast_to(flip_at, value.shape)
            return jnp.take_along_axis(value, at, axis=1)[:rows]

        def extract(tile, rows):
            blank = jnp.zeros((rows, LANES), jnp.float32)
            parts_w, parts_e = [blank] * 4, [blank] * 4
            loaded = {}

            def at(n):
                if n not in loaded:
                    loaded[n] = tile(n)
                return loaded[n]

            for i in range(-1, width):
                pe = width * i + width - 1
                pw = pe + 1
                shift = (i - pe) % LANES
                turned = {}
                for n in {pe // LANES if i >= 0 else pw // LANES, pw // LANES if i + 1 < width else pe // LANES}:
                    turned[n] = roll(at(n), shift)
                if i >= 0:
                    parts_e[i % 4] = jnp.where(lane == i, turned[pe // LANES], parts_e[i % 4])
                if i + 1 < width:
                    parts_w[i % 4] = jnp.where(lane == i + 1, turned[pw // LANES], parts_w[i % 4])
            west = (parts_w[0] + parts_w[1]) + (parts_w[2] + parts_w[3])
            east = (parts_e[0] + parts_e[1]) + (parts_e[2] + parts_e[3])

            def line(start):
                a, n = start % LANES, start // LANES
                if a == 0:
                    return jnp.where(lane < width, at(n), 0.0)
                head = roll(at(n), -a)
                if a + width <= LANES:
                    return jnp.where(lane < width, head, 0.0)
                tail = roll(at(n + 1), -a)
                return jnp.where(lane < LANES - a, head, jnp.where(lane < width, tail, 0.0))

            return west, east, line(0), line(width * (width - 1))

        def insert(west, east, south, north, store):
            even = (lane & 1) == 0
            mixed = (jnp.where(even, east, west), jnp.where(even, west, east))
            tiles_of = {}

            def add(n, mask, value):
                tiles_of.setdefault(n, []).append((mask, value))

            for i in range(-1, width):
                pe = width * i + width - 1
                pw = pe + 1
                turned = roll(mixed[i % 2], (pe - i) % LANES)
                if i >= 0 and i + 1 < width and pe // LANES == pw // LANES:
                    mask = (lane == pe % LANES) | (lane == pw % LANES)
                    add(pe // LANES, mask, turned)
                else:
                    if i >= 0:
                        add(pe // LANES, lane == pe % LANES, turned)
                    if i + 1 < width:
                        add(pw // LANES, lane == pw % LANES, turned)
            extra = {}
            for start, rim in ((0, south), (width * (width - 1), north)):
                a, n = start % LANES, start // LANES
                turned = roll(rim, a)
                extra.setdefault(n, []).append(jnp.where(lane >= a, turned, 0.0) if a else turned)
                if a + width > LANES:
                    extra.setdefault(n + 1, []).append(jnp.where(lane < a + width - LANES, turned, 0.0))
            blank = jnp.zeros(west.shape, jnp.float32)
            for n in range(n_tiles):
                total = blank
                for mask, value in tiles_of.get(n, ()):
                    total = jnp.where(mask, value, total)
                for value in extra.get(n, ()):
                    total = total + value
                store(n, total)

        shift_bits = 22
        factor = (1 << shift_bits) // width + 1
        for c in range(chunks):
            index = lax.broadcasted_iota(jnp.int32, (1, CHUNK), 1) + c * CHUNK
            column = index - width * ((index * factor) >> shift_bits)
            nw_ref[:, pl.ds(c * CHUNK, CHUNK)] = jnp.where(column == 0, 0.0, 1.0)
            ne_ref[:, pl.ds(c * CHUNK, CHUNK)] = jnp.where(column == width - 1, 0.0, 1.0)
        tail = wide - LANES
        m_ref[:, :, :LANES] = jnp.zeros((slots * fields_n, levels, LANES), jnp.float32)
        m_ref[:, :, tail + LANES :] = jnp.zeros((slots * fields_n, levels, 2 * LANES), jnp.float32)
        uv_ref[:, :, :LANES] = jnp.zeros((2, slots, LANES), jnp.float32)
        uv_ref[:, :, tail + LANES :] = jnp.zeros((2, slots, 2 * LANES), jnp.float32)
        for ref in (s_ref, u_ref):
            ref[:, :LANES] = jnp.zeros((slots, LANES), jnp.float32)
            ref[:, wide + LANES :] = jnp.zeros((slots, LANES), jnp.float32)
        w_ref[:, tail:] = jnp.zeros((slots, LANES), jnp.float32)
        d_ref[:, tail:] = jnp.zeros((slots, LANES), jnp.float32)

        def per_level(read):
            level = lax.broadcasted_iota(jnp.int32, (levels, 1), 0)
            value = jnp.zeros((levels, 1), jnp.float32)
            for n in range(levels):
                value = jnp.where(level == n, read(n), value)
            return value

        thick_col = per_level(lambda n: thick[n])
        mix_col = per_level(lambda n: mixing[n])

        copies[0].wait()
        copies[1].wait()
        spans = [(c * CHUNK, min(CHUNK, cells - c * CHUNK)) for c in range(chunks)]
        for at, size in spans:
            w_ref[:, pl.ds(at, size)] = wbuf[:, pl.ds(at, size)].astype(jnp.float32)
            d_ref[:, pl.ds(at, size)] = dbuf[:, pl.ds(at, size)] + 4.0
        for k in range(slots):
            copies[2 + k].wait()
            for f in range(fields_n):
                for at, size in spans:
                    masked = fbuf[k, f, :, pl.ds(at, size)] * w_ref[k : k + 1, pl.ds(at, size)]
                    m_ref[k * fields_n + f, :, pl.ds(LANES + at, size)] = masked
                    if f < 2:
                        uv_ref[f, k : k + 1, pl.ds(LANES + at, size)] = jnp.sum(
                            masked * thick_col, axis=0, keepdims=True
                        )

        for f in range(2):
            for e, rim in enumerate(extract(lambda n: uv_ref[f, :, pl.ds(LANES * (n + 1), LANES)], slots)):
                for k in range(slots):
                    pack1[POS[e], k, f : f + 1, :] = rim[k : k + 1]

        pl.semaphore_wait(barrier, peers)
        sent1 = exchange(pack1, near1, send1, recv1)

        def slab_pack(kf, carry):
            rims = extract(lambda n: m_ref[kf, :, pl.ds(LANES * (n + 1), LANES)], levels)
            for e, rim in enumerate(rims):
                packb[POS[e], kf] = rim
            return carry

        lax.fori_loop(0, slots * fields_n, slab_pack, 0)
        sentb = exchange(packb, nearb, sendb, recvb)

        def entry(k, e):
            dt, ds, p, code = (links[0, 0, k, e, n] for n in range(4))
            source = place(dt, tiles) * n_s + place(ds, strips)
            return source, jnp.maximum(p, 0), p, code

        def choose(number, test, yes, no):
            return jnp.where(test(jnp.full(yes.shape, number, jnp.int32)), yes, no)

        def turn(code):
            a = jnp.where(code == 0, 1.0, jnp.where(code == 2, -1.0, 0.0))
            b = jnp.where(code == 1, 1.0, jnp.where(code == 3, -1.0, 0.0))
            return a, b

        def surface_rims(near):
            for e in range(4):
                for k in range(slots):
                    source, slot, p, code = entry(k, e)
                    rim = near[source, POS[e ^ 1], slot]
                    rim = choose(code, lambda x: x != 0, flip(rim), rim)
                    rim_ref[e, k : k + 1, :] = choose(p, lambda x: x >= 0, rim, jnp.zeros_like(rim))

        def put_edges():
            def store(n, value):
                eb_ref[:, pl.ds(n * LANES, LANES)] = value

            insert(rim_ref[0], rim_ref[1], rim_ref[2], rim_ref[3], store)

        inner = slice(LANES, LANES + CHUNK)

        for copy in sent1:
            copy.wait_recv()
        for e in range(4):
            for k in range(slots):
                source, slot, p, code = entry(k, e)
                pair = near1[source, POS[e ^ 1], slot]
                pair = choose(code, lambda x: x != 0, flip(pair), pair)
                pair = choose(p, lambda x: x >= 0, pair, jnp.zeros_like(pair))
                a, b = turn(code)
                if e < 2:
                    rim = a * pair[0:1] + b * pair[1:2]
                else:
                    rim = a * pair[1:2] - b * pair[0:1]
                rim_ref[e, k : k + 1, :] = rim if e in (1, 3) else -rim
        put_edges()
        for c in range(chunks):
            at = c * CHUNK
            span = pl.ds(at, CHUNK)
            u_win = uv_ref[0, :, pl.ds(at, CHUNK + 2 * LANES)]
            v_win = uv_ref[1, :, pl.ds(at, CHUNK + 2 * LANES)]
            flux = ne_ref[:, span] * roll(u_win, -1)[:, inner] - nw_ref[:, span] * roll(u_win, 1)[:, inner]
            flux = flux + (roll(v_win, -width)[:, inner] - roll(v_win, width)[:, inner]) + eb_ref[:, span]
            s_ref[:, pl.ds(LANES + at, CHUNK)] = w_ref[:, span] * (0.5 * flux)

        def send_surface(x_ref, pack, near, send_sem, recv_sem):
            for e, rim in enumerate(extract(lambda n: x_ref[:, pl.ds(LANES * (n + 1), LANES)], slots)):
                for k in range(slots):
                    pack[POS[e], k, :, :] = rim[k : k + 1]
            return exchange(pack, near, send_sem, recv_sem)

        def image(x_ref, at):
            span = pl.ds(at, CHUNK)
            win = x_ref[:, pl.ds(at, CHUNK + 2 * LANES)]
            near = ne_ref[:, span] * roll(win, -1)[:, inner] + nw_ref[:, span] * roll(win, 1)[:, inner]
            near = near + (roll(win, -width)[:, inner] + roll(win, width)[:, inner]) + eb_ref[:, span]
            return w_ref[:, span] * (d_ref[:, span] * win[:, inner] - near)

        def slab_slot(k):
            for e in range(4):
                source, slot, p, code = entry(k, e)
                a, b = turn(code)
                got = []
                for f in range(fields_n):
                    rim = nearb[source, POS[e ^ 1], slot * fields_n + f]
                    rim = choose(code, lambda x: x != 0, flip(rim), rim)
                    got.append(choose(p, lambda x: x >= 0, rim, jnp.zeros_like(rim)))
                rims_ref[e, 0] = a * got[0] + b * got[1]
                rims_ref[e, 1] = a * got[1] - b * got[0]
                for f in range(2, fields_n):
                    rims_ref[e, f] = got[f]

            def one(f, carry):
                def store(n, value):
                    ebs_ref[:, pl.ds(n * LANES, LANES)] = value

                insert(rims_ref[0, f], rims_ref[1, f], rims_ref[2, f], rims_ref[3, f], store)
                spread_col = per_level(lambda n: spread[f, n])
                for at, size in spans:
                    span = pl.ds(at, CHUNK)
                    win = m_ref[k * fields_n + f, :, pl.ds(at, CHUNK + 2 * LANES)]
                    mid = win[:, inner]
                    flat = ne_ref[:, span] * roll(win, -1)[:, inner] + nw_ref[:, span] * roll(win, 1)[:, inner]
                    flat = flat + (roll(win, -width)[:, inner] + roll(win, width)[:, inner]) + ebs_ref[:, span]
                    flat = flat - 4.0 * mid
                    above = jnp.concatenate([mid[1:], mid[-1:]], 0)
                    below = jnp.concatenate([mid[:1], mid[:-1]], 0)
                    column = above + below - 2.0 * mid
                    new = w_ref[k : k + 1, span] * (mid + spread_col * flat + mix_col * column)
                    fbuf[k, f, :, pl.ds(at, size)] = new[:, :size]
                return carry

            lax.fori_loop(0, fields_n, one, 0)
            copy = pltpu.make_async_copy(fbuf.at[k], out_f.at[0, 0, k], out_sem.at[k])
            copy.start()
            return copy

        def slab_part(part):
            return [slab_slot(k) for k in range(slots) if k * 3 // slots == part]

        sent2 = send_surface(s_ref, pack2, near2, send2, recv2)
        for copy in sentb:
            copy.wait_recv()
        put_out = slab_part(0)
        for copy in sent2:
            copy.wait_recv()
        surface_rims(near2)
        put_edges()
        for c in range(chunks):
            u_ref[:, pl.ds(LANES + c * CHUNK, CHUNK)] = image(s_ref, c * CHUNK)
        sent3 = send_surface(u_ref, pack3, near3, send3, recv3)
        put_out += slab_part(1)
        for copy in sent3:
            copy.wait_recv()
        surface_rims(near3)
        put_edges()
        blank = jnp.zeros((slots, CHUNK), jnp.float32)

        def whole(value):
            return jnp.sum(jnp.sum(value, axis=1, keepdims=True), axis=0, keepdims=True)

        ss = su = uu = uv = blank
        for c in range(chunks):
            x = s_ref[:, pl.ds(LANES + c * CHUNK, CHUNK)]
            y = u_ref[:, pl.ds(LANES + c * CHUNK, CHUNK)]
            z = image(u_ref, c * CHUNK)
            v_ref[:, pl.ds(c * CHUNK, CHUNK)] = z
            ss, su, uu, uv = ss + x * x, su + x * y, uu + y * y, uv + y * z
        ss, su, uu, uv = whole(ss), whole(su), whole(uu), whole(uv)
        ratio = jnp.where(su > 0.0, ss / su, 0.0)
        ee = eu = ef = uf = blank
        for c in range(chunks):
            x = s_ref[:, pl.ds(LANES + c * CHUNK, CHUNK)]
            y = u_ref[:, pl.ds(LANES + c * CHUNK, CHUNK)]
            z = v_ref[:, pl.ds(c * CHUNK, CHUNK)]
            left = x - ratio * y
            left_image = y - ratio * z
            ee, eu, ef = ee + left * left, eu + left * y, ef + left * left_image
            uf = uf + (y * left_image + left * z)
        row = jnp.zeros((1, LANES), jnp.float32)
        for n, value in enumerate((ss, su, ratio, whole(ee), whole(eu), uu, whole(ef), whole(uf), uv)):
            row = jnp.where(lane == n, value, row)
        row_ref[...] = row
        red_ref[me_first] = row

        def first_copy(j):
            other = lax.rem(me_first + j, first)
            return pltpu.make_async_remote_copy(
                src_ref=row_ref,
                dst_ref=red_ref.at[me_first],
                send_sem=sendr.at[j],
                recv_sem=recvr.at[me_first],
                device_id=(base + other // strips, other % strips),
                device_id_type=pl.DeviceIdType.MESH,
            )

        def first_arrival(j):
            other = lax.rem(me_first + j, first)
            return pltpu.make_async_remote_copy(
                src_ref=row_ref,
                dst_ref=red_ref.at[other],
                send_sem=sendr.at[j],
                recv_sem=recvr.at[other],
                device_id=(base + other // strips, other % strips),
                device_id_type=pl.DeviceIdType.MESH,
            )

        for j in range(1, first):
            first_copy(j).start()
        put_out += slab_part(2)
        for j in range(1, first):
            first_arrival(j).wait_recv()

        if high > 1:
            mine = t // low
            copies2 = []
            for j in range(1, high):
                other = lax.rem(mine + j, high)
                copy = pltpu.make_async_remote_copy(
                    src_ref=red_ref,
                    dst_ref=red2_ref.at[mine],
                    send_sem=sendq.at[j],
                    recv_sem=recvq.at[mine],
                    device_id=(other * low + place_t, s),
                    device_id_type=pl.DeviceIdType.MESH,
                )
                copy.start()
                copies2.append(copy)
            red2_ref[mine] = red_ref[...]
            for j in range(1, high):
                other = lax.rem(mine + j, high)
                pltpu.make_async_remote_copy(
                    src_ref=red_ref,
                    dst_ref=red2_ref.at[other],
                    send_sem=sendq.at[j],
                    recv_sem=recvq.at[other],
                    device_id=(other * low + place_t, s),
                    device_id_type=pl.DeviceIdType.MESH,
                ).wait_recv()
            for copy in copies2:
                copy.wait_send()
            rows = [red2_ref[n] for n in range(high)]
        else:
            rows = [red_ref[...]]

        total = sum(jnp.sum(x, axis=0) for x in rows)
        rr0, sas = total[:, 0:1], total[:, 1:2]
        alpha0 = rr0 / sas
        moved = jnp.zeros((1, LANES), jnp.float32)
        lane3 = lax.broadcasted_iota(jnp.int32, (1, 1, LANES), 2)
        for x in rows:
            delta = jnp.broadcast_to(x[:, :, 2:3], x.shape) - alpha0[None]
            weight = jnp.where(
                (lane3 == 3) | (lane3 == 6), 1.0,
                jnp.where(lane3 == 4, 2.0 * delta, jnp.where(lane3 == 7, delta, delta * delta)),
            )
            moved = moved + jnp.sum(x * weight, axis=0)
        rr1 = jnp.sum(jnp.where((lane >= 3) & (lane <= 5), moved, 0.0), axis=1, keepdims=True)
        rar = jnp.sum(jnp.where((lane >= 6) & (lane <= 8), moved, 0.0), axis=1, keepdims=True)
        beta = rr1 / rr0
        alpha1 = rr1 / (rar - beta * rr1 / alpha0)
        for at, size in spans:
            x = s_ref[:, pl.ds(LANES + at, CHUNK)]
            y = u_ref[:, pl.ds(LANES + at, CHUNK)]
            z = v_ref[:, pl.ds(at, CHUNK)]
            r1 = x - alpha0 * y
            direction = r1 + beta * x
            direction_image = (y - alpha0 * z) + beta * y
            out_x[0, 0, :, pl.ds(at, size)] = (alpha0 * x + alpha1 * direction)[:, :size]
            out_r[0, 0, :, pl.ds(at, size)] = (r1 - alpha1 * direction_image)[:, :size]

        for copy in sent1 + sentb + sent2 + sent3:
            copy.wait_send()
        for j in range(1, first):
            first_copy(j).wait_send()
        for copy in put_out:
            copy.wait()

    f32 = jnp.float32
    any_space = pl.BlockSpec(memory_space=pl.ANY)
    smem = pl.BlockSpec(memory_space=pltpu.SMEM)
    vmem = pl.BlockSpec(memory_space=pltpu.VMEM)
    kf = slots * fields_n
    dma = pltpu.SemaphoreType.DMA
    return pl.pallas_call(
        kernel,
        out_shape=(
            jax.ShapeDtypeStruct((1, 1, slots, fields_n, levels, cells), f32),
            jax.ShapeDtypeStruct((1, 1, slots, cells), f32),
            jax.ShapeDtypeStruct((1, 1, slots, cells), f32),
        ),
        in_specs=[any_space, any_space, smem, any_space, smem, smem, smem],
        out_specs=(any_space, vmem, vmem),
        scratch_shapes=[
            pltpu.VMEM((slots, fields_n, levels, cells), f32),
            pltpu.VMEM((slots, cells), jnp.int32),
            pltpu.VMEM((slots, cells), f32),
            pltpu.VMEM((kf, levels, padded), f32),
            pltpu.VMEM((slots, wide), f32),
            pltpu.VMEM((slots, wide), f32),
            pltpu.VMEM((1, wide), f32),
            pltpu.VMEM((1, wide), f32),
            pltpu.VMEM((2, slots, padded), f32),
            pltpu.VMEM((slots, padded), f32),
            pltpu.VMEM((slots, padded), f32),
            pltpu.VMEM((slots, wide), f32),
            pltpu.VMEM((slots, wide), f32),
            pltpu.VMEM((levels, wide), f32),
            pltpu.VMEM((4, slots, LANES), f32),
            pltpu.VMEM((4, fields_n, levels, LANES), f32),
            pltpu.VMEM((4, slots, 2, LANES), f32),
            pltpu.VMEM((n_dirs, 4, slots, 2, LANES), f32),
            pltpu.VMEM((4, kf, levels, LANES), f32),
            pltpu.VMEM((n_dirs, 4, kf, levels, LANES), f32),
            pltpu.VMEM((4, slots, 1, LANES), f32),
            pltpu.VMEM((n_dirs, 4, slots, 1, LANES), f32),
            pltpu.VMEM((4, slots, 1, LANES), f32),
            pltpu.VMEM((n_dirs, 4, slots, 1, LANES), f32),
            pltpu.VMEM((1, LANES), f32),
            pltpu.VMEM((first, 1, LANES), f32),
            pltpu.VMEM((high, first, 1, LANES) if high > 1 else (1, 1, 1, LANES), f32),
            dma((2 + slots,)),
            dma((slots,)),
            dma((n_dirs,)), dma((n_dirs,)), dma((n_dirs,)), dma((n_dirs,)),
            dma((n_dirs,)), dma((n_dirs,)), dma((n_dirs,)), dma((n_dirs,)),
            dma((first,)), dma((first,)), dma((high,)), dma((high,)),
        ],
        compiler_params=pltpu.CompilerParams(collective_id=0, has_side_effects=True),
    )


def solution(mesh):
    tiles, strips = mesh.shape["tiles"], mesh.shape["strip"]

    def on_device(fields, wet_land, links, surface_diagonal, spread, mixing, thickness):
        slots, fields_n, levels, cells = fields.shape[2:]
        call = build(tiles, strips, slots, fields_n, levels, cells)
        return call(fields, wet_land, links, surface_diagonal, spread, mixing, thickness)

    placed = (
        P("tiles", "strip", None, None, None, None),
        P("tiles", "strip", None, None),
        P("tiles", "strip", None, None, None),
        P("tiles", "strip", None, None),
        P(),
        P(),
        P(),
    )
    return jax.shard_map(
        on_device,
        mesh=mesh,
        in_specs=placed,
        out_specs=(
            P("tiles", "strip", None, None, None, None),
            P("tiles", "strip", None, None),
            P("tiles", "strip", None, None),
        ),
        check_vma=False,
    )
```

time: 162 us -> 38 us (0.23)
  blocking collectives: 76 us -> 0 us
  Pallas kernels: 0 us -> 28.1 us
  starting transfers between devices: 21.2 us -> 0 us
  local copies, waits for them, and re-layouts: 29.6 us -> 8.89 us
  waiting for transfers between devices: 14.1 us -> 0 us
  other arithmetic: 13.9 us -> 0 us
  between operations: 7.01 us -> 0.64 us
    psum x2 -> x0, blocking collectives: 76 us -> none  [paired_totals(): lax.psum((jnp.sum(residual * residual), jnp.sum(residual * image)), ('til...]
    pallas_call x0 -> x1, Pallas kernels: none -> 28.1 us  [on_device(): call(fields, wet_land, links, surface_diagonal, spread, mixing, thickness)]
    ppermute x12 -> x0, starting transfers between devices: 21.2 us -> none  [the longest x6 14.3 us: extended(): after = lax.ppermute(leading, axis, down)]
    ppermute x12 -> x0, waiting for transfers between devices: 14.1 us -> none  [the longest x6 8.48 us: extended(): before = lax.ppermute(last, axis, up)]
    reshape x16 -> x0, local copies, waits for them, and re-layouts: 12.5 us -> none  [the longest x3 2.95 us: beside_values(): jnp.broadcast_to(rims[..., 0, :, None], leading + (width, width))]
    slice x19 -> x0, local copies, waits for them, and re-layouts: 11 us -> none  [the longest x2 3.3 us: slab_step(): below = jnp.concatenate([masked[..., :1, :], masked[..., :-1, :]], axis=-2)]
    broadcast_in_dim x4 -> x0, other arithmetic: 7.53 us -> none  [the longest x1 7.25 us: on_device(): return (updated[None, None], solution[None, None], residual[None, None])]
    unnamed x24 -> x3, local copies, waits for them, and re-layouts: 0.46 us -> 5.6 us
  transfers between devices with their start and end apart: 12 -> 0, of which waited for: 8 -> 0; matrix products, arithmetic and copies ran while one was open for 5% -> 0% of each run, Pallas kernels for 0% -> 0%
where the time goes in v1:
time: 38 us; the launch traced here: 37.7 us
  Pallas kernels  28.1 us (74%)
  local copies, waits for them, and re-layouts  8.89 us (23%)
  between operations  0.64 us (2%)
    pallas_call x1, Pallas kernels, on_device(): call(fields, wet_land, links, surface_diagonal, spread, mixing, thickness)  28.1 us
    unnamed x3, local copies, waits for them, and re-layouts  5.6 us
    pallas_call x2, local copies, waits for them, and re-layouts, on_device(): call(fields, wet_land, links, surface_diagonal, spread, mixing, thickness)  3.29 us

profile of v1, /device:TPU:0, one launch (start us, length us, event | category | flops | bytes accessed | tf_op | source)
XLA Modules:
  0.0 37.7 jit_solution(10916009255516462298)
XLA Ops:
  0.6 1.6 %copy.10.wet_in = s32[1,1,3,8100]{3,2,1,0:T(4,128)} copy(s32[1,1,3,8100]{3,1,2,0:T(1,128)} %param.8) | data formatting | bytes 194400 | tf_op args[1]
  2.2 1.6 %copy.11.diag_in = f32[1,1,3,8100]{3,2,1,0:T(4,128)} copy(f32[1,1,3,8100]{3,1,2,0:T(1,128)} %param.10) | data formatting | bytes 194400 | tf_op args[3]
  3.9 28.1 %shard_map.94 = (f32[1,1,3,3,4,8100]{5,4,3,2,1,0:T(4,128)}, f32[1,1,3,8100]{3,2,1,0:T(4,128)}, f32[1,1,3,8100]{3,2,1,0:T(4,128)}) custom-call(f32[1,1,3,3,4,8100]{5,4,3,2,1,0:T(4,128)} %fields.1, s32[1,1,3,8100]{3,2,1,0:T(4,128)} %copy.10.wet_in, s32[1,1,3,4,4]{4,3,2,1,0:T(4,128)} %links.1, f32[1,1,3,8100]{3,2,1,0:T(4,128)} %copy.11.diag_in, f32[3,4]{1,0:T(4,128)} %spread.1, ...), custom_call_target="tpu_custom_call" | custom-call | tf_op jit(solution)/shard_map/pallas_call | solution.py:568
  32.0 1.6 %copy.12 = f32[1,1,3,8100]{3,1,2,0:T(1,128)} copy(f32[1,1,3,8100]{3,2,1,0:T(4,128)} %get-tuple-element.4) | data formatting | bytes 194400 | tf_op jit(solution)/shard_map/pallas_call | solution.py:568
  33.6 1.6 %copy.13 = f32[1,1,3,8100]{3,1,2,0:T(1,128)} copy(f32[1,1,3,8100]{3,2,1,0:T(4,128)} %get-tuple-element.5) | data formatting | bytes 194400 | tf_op jit(solution)/shard_map/pallas_call | solution.py:568
  35.3 2.4 %copy.15 = f32[1,1,3,3,4,8100]{5,4,3,2,1,0:T(4,128)} copy(f32[1,1,3,3,4,8100]{5,4,3,2,1,0:T(4,128)} %get-tuple-element.9) | data formatting | bytes 2332800

commit v2 on v1

--- a/solution.py
+++ b/solution.py
@@ -60,18 +60,24 @@
             directions.append((dt, ds, here, back, min(sides), max(sides) + 1))
 
     def kernel(
-        fields, wet_in, links, diag_in, spread, mixing, thick, out_f, out_x, out_r,
-        fbuf, wbuf, dbuf, m_ref, w_ref, d_ref, nw_ref, ne_ref, uv_ref, s_ref, u_ref, v_ref, eb_ref, ebs_ref,
+        fields, wet_in, links_in, diag_in, spread_in, mixing_in, thick_in, out_f, out_x, out_r,
+        links, spread, mixing, thick, fbuf, wbuf, dbuf, m_ref, w_ref, d_ref, nw_ref, ne_ref, uv_ref, s_ref, u_ref, v_ref, eb_ref, ebs_ref,
         rim_ref, rims_ref, pack1, near1, packb, nearb, pack2, near2, pack3, near3, row_ref, red_ref, red2_ref,
-        in_sem, out_sem, send1, recv1, sendb, recvb, send2, recv2, send3, recv3, sendr, recvr, sendq, recvq,
+        in_sem, send1, recv1, sendb, recvb, send2, recv2, send3, recv3, sendr, recvr, sendq, recvq,
     ):
         t = lax.axis_index("tiles")
         s = lax.axis_index("strip")
         copies = [
-            pltpu.make_async_copy(wet_in.at[0, 0], wbuf, in_sem.at[0]),
-            pltpu.make_async_copy(diag_in.at[0, 0], dbuf, in_sem.at[1]),
+            pltpu.make_async_copy(wet_in.at[0], wbuf, in_sem.at[0]),
+            pltpu.make_async_copy(diag_in.at[0], dbuf, in_sem.at[1]),
         ] + [pltpu.make_async_copy(fields.at[0, 0, k], fbuf.at[k], in_sem.at[2 + k]) for k in range(slots)]
-        for copy in copies:
+        small = [
+            pltpu.make_async_copy(thick_in, thick, in_sem.at[2 + slots]),
+            pltpu.make_async_copy(mixing_in, mixing, in_sem.at[3 + slots]),
+            pltpu.make_async_copy(spread_in, spread, in_sem.at[4 + slots]),
+            pltpu.make_async_copy(links_in.at[0, 0], links, in_sem.at[5 + slots]),
+        ]
+        for copy in copies[:3] + small + copies[3:]:
             copy.start()
 
         barrier = pltpu.get_barrier_semaphore()
@@ -223,15 +229,18 @@
                 value = jnp.where(level == n, read(n), value)
             return value
 
+        for copy in small:
+            copy.wait()
         thick_col = per_level(lambda n: thick[n])
         mix_col = per_level(lambda n: mixing[n])
 
         copies[0].wait()
         copies[1].wait()
         spans = [(c * CHUNK, min(CHUNK, cells - c * CHUNK)) for c in range(chunks)]
-        for at, size in spans:
-            w_ref[:, pl.ds(at, size)] = wbuf[:, pl.ds(at, size)].astype(jnp.float32)
-            d_ref[:, pl.ds(at, size)] = dbuf[:, pl.ds(at, size)] + 4.0
+        for k in range(slots):
+            for at, size in spans:
+                w_ref[k : k + 1, pl.ds(at, size)] = wbuf[k, :, pl.ds(at, size)].astype(jnp.float32)
+                d_ref[k : k + 1, pl.ds(at, size)] = dbuf[k, :, pl.ds(at, size)] + 4.0
         for k in range(slots):
             copies[2 + k].wait()
             for f in range(fields_n):
@@ -261,7 +270,7 @@
         sentb = exchange(packb, nearb, sendb, recvb)
 
         def entry(k, e):
-            dt, ds, p, code = (links[0, 0, k, e, n] for n in range(4))
+            dt, ds, p, code = (links[k, e, n] for n in range(4))
             source = place(dt, tiles) * n_s + place(ds, strips)
             return source, jnp.maximum(p, 0), p, code
 
@@ -357,21 +366,20 @@
                     below = jnp.concatenate([mid[:1], mid[:-1]], 0)
                     column = above + below - 2.0 * mid
                     new = w_ref[k : k + 1, span] * (mid + spread_col * flat + mix_col * column)
-                    fbuf[k, f, :, pl.ds(at, size)] = new[:, :size]
+                    out_f[0, 0, k, f, :, pl.ds(at, size)] = new[:, :size]
                 return carry
 
             lax.fori_loop(0, fields_n, one, 0)
-            copy = pltpu.make_async_copy(fbuf.at[k], out_f.at[0, 0, k], out_sem.at[k])
-            copy.start()
-            return copy
 
         def slab_part(part):
-            return [slab_slot(k) for k in range(slots) if k * 3 // slots == part]
+            for k in range(slots):
+                if k * 3 // slots == part:
+                    slab_slot(k)
 
         sent2 = send_surface(s_ref, pack2, near2, send2, recv2)
         for copy in sentb:
             copy.wait_recv()
-        put_out = slab_part(0)
+        slab_part(0)
         for copy in sent2:
             copy.wait_recv()
         surface_rims(near2)
@@ -379,7 +387,7 @@
         for c in range(chunks):
             u_ref[:, pl.ds(LANES + c * CHUNK, CHUNK)] = image(s_ref, c * CHUNK)
         sent3 = send_surface(u_ref, pack3, near3, send3, recv3)
-        put_out += slab_part(1)
+        slab_part(1)
         for copy in sent3:
             copy.wait_recv()
         surface_rims(near3)
@@ -437,7 +445,7 @@
 
         for j in range(1, first):
             first_copy(j).start()
-        put_out += slab_part(2)
+        slab_part(2)
         for j in range(1, first):
             first_arrival(j).wait_recv()
 
@@ -496,35 +504,40 @@
             r1 = x - alpha0 * y
             direction = r1 + beta * x
             direction_image = (y - alpha0 * z) + beta * y
-            out_x[0, 0, :, pl.ds(at, size)] = (alpha0 * x + alpha1 * direction)[:, :size]
-            out_r[0, 0, :, pl.ds(at, size)] = (r1 - alpha1 * direction_image)[:, :size]
+            answer = alpha0 * x + alpha1 * direction
+            left = r1 - alpha1 * direction_image
+            for k in range(slots):
+                out_x[0, k, :, pl.ds(at, size)] = answer[k : k + 1, :size]
+                out_r[0, k, :, pl.ds(at, size)] = left[k : k + 1, :size]
 
         for copy in sent1 + sentb + sent2 + sent3:
             copy.wait_send()
         for j in range(1, first):
             first_copy(j).wait_send()
-        for copy in put_out:
-            copy.wait()
 
     f32 = jnp.float32
     any_space = pl.BlockSpec(memory_space=pl.ANY)
-    smem = pl.BlockSpec(memory_space=pltpu.SMEM)
+    hbm = pl.BlockSpec(memory_space=pltpu.HBM)
     vmem = pl.BlockSpec(memory_space=pltpu.VMEM)
     kf = slots * fields_n
     dma = pltpu.SemaphoreType.DMA
     return pl.pallas_call(
         kernel,
         out_shape=(
-            jax.ShapeDtypeStruct((1, 1, slots, fields_n, levels, cells), f32),
-            jax.ShapeDtypeStruct((1, 1, slots, cells), f32),
-            jax.ShapeDtypeStruct((1, 1, slots, cells), f32),
+            pltpu.VMEM((1, 1, slots, fields_n, levels, cells), f32),
+            pltpu.VMEM((1, slots, 1, cells), f32),
+            pltpu.VMEM((1, slots, 1, cells), f32),
         ),
-        in_specs=[any_space, any_space, smem, any_space, smem, smem, smem],
-        out_specs=(any_space, vmem, vmem),
+        in_specs=[hbm] * 7,
+        out_specs=(vmem, vmem, vmem),
         scratch_shapes=[
+            pltpu.SMEM((slots, 4, 4), jnp.int32),
+            pltpu.SMEM((fields_n, levels), f32),
+            pltpu.SMEM((levels,), f32),
+            pltpu.SMEM((levels,), f32),
             pltpu.VMEM((slots, fields_n, levels, cells), f32),
-            pltpu.VMEM((slots, cells), jnp.int32),
-            pltpu.VMEM((slots, cells), f32),
+            pltpu.VMEM((slots, 1, cells), jnp.int32),
+            pltpu.VMEM((slots, 1, cells), f32),
             pltpu.VMEM((kf, levels, padded), f32),
             pltpu.VMEM((slots, wide), f32),
             pltpu.VMEM((slots, wide), f32),
@@ -549,14 +562,35 @@
             pltpu.VMEM((1, LANES), f32),
             pltpu.VMEM((first, 1, LANES), f32),
             pltpu.VMEM((high, first, 1, LANES) if high > 1 else (1, 1, 1, LANES), f32),
-            dma((2 + slots,)),
-            dma((slots,)),
+            dma((6 + slots,)),
             dma((n_dirs,)), dma((n_dirs,)), dma((n_dirs,)), dma((n_dirs,)),
             dma((n_dirs,)), dma((n_dirs,)), dma((n_dirs,)), dma((n_dirs,)),
             dma((first,)), dma((first,)), dma((high,)), dma((high,)),
         ],
-        compiler_params=pltpu.CompilerParams(collective_id=0, has_side_effects=True),
+        compiler_params=pltpu.CompilerParams(
+            collective_id=0, has_side_effects=True, vmem_limit_bytes=58 << 20
+        ),
     )
+
+
+def put(*arrays):
+    def kernel(*refs):
+        count = len(arrays)
+        sems = refs[-1]
+        copies = [pltpu.make_async_copy(refs[n], refs[count + n], sems.at[n]) for n in range(count)]
+        for copy in copies:
+            copy.start()
+        for copy in copies:
+            copy.wait()
+
+    return pl.pallas_call(
+        kernel,
+        out_shape=tuple(jax.ShapeDtypeStruct(x.shape, x.dtype) for x in arrays),
+        in_specs=[pl.BlockSpec(memory_space=pl.ANY)] * len(arrays),
+        out_specs=tuple(pl.BlockSpec(memory_space=pltpu.HBM) for _ in arrays),
+        scratch_shapes=[pltpu.SemaphoreType.DMA((len(arrays),))],
+        compiler_params=pltpu.CompilerParams(vmem_limit_bytes=1 << 20),
+    )(*arrays)
 
 
 def solution(mesh):
@@ -565,7 +599,10 @@
     def on_device(fields, wet_land, links, surface_diagonal, spread, mixing, thickness):
         slots, fields_n, levels, cells = fields.shape[2:]
         call = build(tiles, strips, slots, fields_n, levels, cells)
-        return call(fields, wet_land, links, surface_diagonal, spread, mixing, thickness)
+        wet_land, surface_diagonal = (jnp.swapaxes(x, 1, 2) for x in (wet_land, surface_diagonal))
+        new, answer, left = call(fields, wet_land, links, surface_diagonal, spread, mixing, thickness)
+        new, answer, left = put(new, answer, left)
+        return new, jnp.swapaxes(answer, 1, 2), jnp.swapaxes(left, 1, 2)
 
     placed = (
         P("tiles", "strip", None, None, None, None),

time: 38 us -> 28.5 us (0.75)
  local copies, waits for them, and re-layouts: 8.89 us -> 0 us
  Pallas kernels: 28.1 us -> 27.7 us
    unnamed x3 -> x0, local copies, waits for them, and re-layouts: 5.6 us -> none
    pallas_call x2 -> x0, local copies, waits for them, and re-layouts: 3.29 us -> none  [on_device(): call(fields, wet_land, links, surface_diagonal, spread, mixing, thickness)]
    pallas_call x1, Pallas kernels: 28.1 us -> 26.7 us  [on_device(): call(fields, wet_land, links, surface_diagonal, spread, mixing, thickness)]
    pallas_call x0 -> x1, Pallas kernels: none -> 1.09 us  [put(): pl.pallas_call(kernel, out_shape=tuple((jax.ShapeDtypeStruct(x.shape, x.d...]
where the time goes in v2:
time: 28.5 us; the launch traced here: 28.4 us
  Pallas kernels  27.7 us (97%)
  between operations  0.64 us (2%)
    pallas_call x1, Pallas kernels, on_device(): call(fields, wet_land, links, surface_diagonal, spread, mixing, thickness)  26.7 us
    pallas_call x1, Pallas kernels, put(): pl.pallas_call(kernel, out_shape=tuple((jax.ShapeDtypeStruct(x.shape, x.d...  1.09 us

profile of v2, /device:TPU:0, one launch (start us, length us, event | category | flops | bytes accessed | tf_op | source)
XLA Modules:
  0.0 28.4 jit_solution(15075623511265394348)
XLA Ops:
  0.6 26.7 %shard_map.94 = (f32[1,1,3,3,4,8100]{5,4,3,2,1,0:T(4,128)S(1)}, f32[1,3,1,8100]{3,2,1,0:T(1,128)S(1)}, f32[1,3,1,8100]{3,2,1,0:T(1,128)S(1)}) custom-call(f32[1,1,3,3,4,8100]{5,4,3,2,1,0:T(4,128)} %fields.1, s32[1,3,1,8100]{3,2,1,0:T(1,128)} %bitcast.8, s32[1,1,3,4,4]{4,3,2,1,0:T(4,128)} %links_in.1, f32[1,3,1,8100]{3,2,1,0:T(1,128)} %bitcast.9, ...), custom_call_target="tpu_custom_call" | custom-call | tf_op jit(solution)/shard_map/pallas_call | solution.py:603
  27.3 1.1 %shard_map.95 = (f32[1,1,3,3,4,8100]{5,4,3,2,1,0:T(4,128)}, f32[1,3,1,8100]{3,2,1,0:T(1,128)}, f32[1,3,1,8100]{3,2,1,0:T(1,128)}) custom-call(f32[1,1,3,3,4,8100]{5,4,3,2,1,0:T(4,128)S(1)} %get-tuple-element.9.refs_0_, f32[1,3,1,8100]{3,2,1,0:T(1,128)S(1)} %get-tuple-element.10.refs_1_, f32[1,3,1,8100]{3,2,1,0:T(1,128)S(1)} %get-tuple-element.11.refs_2_), custom_call_target="tpu_custom_call" | custom-call | tf_op jit(solution)/shard_map/pallas_call | solution.py:586

commit v3 on v2

--- a/solution.py
+++ b/solution.py
@@ -296,43 +296,36 @@
 
             insert(rim_ref[0], rim_ref[1], rim_ref[2], rim_ref[3], store)
 
-        inner = slice(LANES, LANES + CHUNK)
-
-        for copy in sent1:
-            copy.wait_recv()
-        for e in range(4):
-            for k in range(slots):
-                source, slot, p, code = entry(k, e)
-                pair = near1[source, POS[e ^ 1], slot]
-                pair = choose(code, lambda x: x != 0, flip(pair), pair)
-                pair = choose(p, lambda x: x >= 0, pair, jnp.zeros_like(pair))
-                a, b = turn(code)
-                if e < 2:
-                    rim = a * pair[0:1] + b * pair[1:2]
-                else:
-                    rim = a * pair[1:2] - b * pair[0:1]
-                rim_ref[e, k : k + 1, :] = rim if e in (1, 3) else -rim
-        put_edges()
-        for c in range(chunks):
-            at = c * CHUNK
-            span = pl.ds(at, CHUNK)
-            u_win = uv_ref[0, :, pl.ds(at, CHUNK + 2 * LANES)]
-            v_win = uv_ref[1, :, pl.ds(at, CHUNK + 2 * LANES)]
-            flux = ne_ref[:, span] * roll(u_win, -1)[:, inner] - nw_ref[:, span] * roll(u_win, 1)[:, inner]
-            flux = flux + (roll(v_win, -width)[:, inner] - roll(v_win, width)[:, inner]) + eb_ref[:, span]
-            s_ref[:, pl.ds(LANES + at, CHUNK)] = w_ref[:, span] * (0.5 * flux)
-
-        def send_surface(x_ref, pack, near, send_sem, recv_sem):
-            for e, rim in enumerate(extract(lambda n: x_ref[:, pl.ds(LANES * (n + 1), LANES)], slots)):
+        def side_totals():
+            west, east, south, north = (rim_ref[e] for e in range(4))
+            end = slice(width - 1, width)
+
+            def ends(at_first, at_last):
+                return jnp.where(lane == 0, at_first, jnp.where(lane == width - 1, at_last, 0.0))
+
+            return (
+                west + ends(south[:, :1], north[:, :1]),
+                east + ends(south[:, end], north[:, end]),
+                south + ends(west[:, :1], east[:, :1]),
+                north + ends(west[:, end], east[:, end]),
+            )
+
+        def send_rims(rims, pack, near, send_sem, recv_sem):
+            for e, rim in enumerate(rims):
                 for k in range(slots):
                     pack[POS[e], k, :, :] = rim[k : k + 1]
             return exchange(pack, near, send_sem, recv_sem)
+
+        def rims_of(x_ref, lead):
+            return extract(lambda n: x_ref[:, pl.ds(LANES * n + lead, LANES)], slots)
+
+        inner = slice(LANES, LANES + CHUNK)
 
         def image(x_ref, at):
             span = pl.ds(at, CHUNK)
             win = x_ref[:, pl.ds(at, CHUNK + 2 * LANES)]
             near = ne_ref[:, span] * roll(win, -1)[:, inner] + nw_ref[:, span] * roll(win, 1)[:, inner]
-            near = near + (roll(win, -width)[:, inner] + roll(win, width)[:, inner]) + eb_ref[:, span]
+            near = near + (roll(win, -width)[:, inner] + roll(win, width)[:, inner])
             return w_ref[:, span] * (d_ref[:, span] * win[:, inner] - near)
 
         def slab_slot(k):
@@ -376,22 +369,55 @@
                 if k * 3 // slots == part:
                     slab_slot(k)
 
-        sent2 = send_surface(s_ref, pack2, near2, send2, recv2)
+        wet_rims = rims_of(w_ref, 0)
+        for c in range(chunks):
+            at = c * CHUNK
+            span = pl.ds(at, CHUNK)
+            u_win = uv_ref[0, :, pl.ds(at, CHUNK + 2 * LANES)]
+            v_win = uv_ref[1, :, pl.ds(at, CHUNK + 2 * LANES)]
+            flux = ne_ref[:, span] * roll(u_win, -1)[:, inner] - nw_ref[:, span] * roll(u_win, 1)[:, inner]
+            flux = flux + (roll(v_win, -width)[:, inner] - roll(v_win, width)[:, inner])
+            s_ref[:, pl.ds(LANES + at, CHUNK)] = w_ref[:, span] * (0.5 * flux)
+        own = rims_of(s_ref, LANES)
+
+        for copy in sent1:
+            copy.wait_recv()
+        for e in range(4):
+            for k in range(slots):
+                source, slot, p, code = entry(k, e)
+                pair = near1[source, POS[e ^ 1], slot]
+                pair = choose(code, lambda x: x != 0, flip(pair), pair)
+                pair = choose(p, lambda x: x >= 0, pair, jnp.zeros_like(pair))
+                a, b = turn(code)
+                if e < 2:
+                    rim = a * pair[0:1] + b * pair[1:2]
+                else:
+                    rim = a * pair[1:2] - b * pair[0:1]
+                rim_ref[e, k : k + 1, :] = (0.5 if e in (1, 3) else -0.5) * rim
+        s_rims = [x + w * y for x, w, y in zip(own, wet_rims, side_totals())]
+        sent2 = send_rims(s_rims, pack2, near2, send2, recv2)
+
+        put_edges()
+        for c in range(chunks):
+            span, shifted = pl.ds(c * CHUNK, CHUNK), pl.ds(LANES + c * CHUNK, CHUNK)
+            s_ref[:, shifted] = s_ref[:, shifted] + w_ref[:, span] * eb_ref[:, span]
+        for c in range(chunks):
+            u_ref[:, pl.ds(LANES + c * CHUNK, CHUNK)] = image(s_ref, c * CHUNK)
+        own = rims_of(u_ref, LANES)
         for copy in sentb:
             copy.wait_recv()
         slab_part(0)
+
         for copy in sent2:
             copy.wait_recv()
         surface_rims(near2)
+        u_rims = [x - w * y for x, w, y in zip(own, wet_rims, side_totals())]
+        sent3 = send_rims(u_rims, pack3, near3, send3, recv3)
+
         put_edges()
         for c in range(chunks):
-            u_ref[:, pl.ds(LANES + c * CHUNK, CHUNK)] = image(s_ref, c * CHUNK)
-        sent3 = send_surface(u_ref, pack3, near3, send3, recv3)
-        slab_part(1)
-        for copy in sent3:
-            copy.wait_recv()
-        surface_rims(near3)
-        put_edges()
+            span, shifted = pl.ds(c * CHUNK, CHUNK), pl.ds(LANES + c * CHUNK, CHUNK)
+            u_ref[:, shifted] = u_ref[:, shifted] - w_ref[:, span] * eb_ref[:, span]
         blank = jnp.zeros((slots, CHUNK), jnp.float32)
 
         def whole(value):
@@ -418,6 +444,21 @@
         row = jnp.zeros((1, LANES), jnp.float32)
         for n, value in enumerate((ss, su, ratio, whole(ee), whole(eu), uu, whole(ef), whole(uf), uv)):
             row = jnp.where(lane == n, value, row)
+        slab_part(1)
+
+        for copy in sent3:
+            copy.wait_recv()
+        surface_rims(near3)
+        edge_u = edge_left = jnp.zeros((slots, LANES), jnp.float32)
+        for e in range(4):
+            got = rim_ref[e]
+            edge_u = edge_u + u_rims[e] * got
+            edge_left = edge_left + (s_rims[e] - ratio * u_rims[e]) * got
+        edge_u, edge_left = whole(edge_u), whole(edge_left)
+        row = row + jnp.where(
+            lane == 6, ratio * edge_left,
+            jnp.where(lane == 7, ratio * edge_u - edge_left, jnp.where(lane == 8, -edge_u, 0.0)),
+        )
         row_ref[...] = row
         red_ref[me_first] = row
 
@@ -443,8 +484,12 @@
                 device_id_type=pl.DeviceIdType.MESH,
             )
 
-        for j in range(1, first):
+        for j in sorted(range(1, first), key=lambda j: abs(2 * j - first)):
             first_copy(j).start()
+        put_edges()
+        for c in range(chunks):
+            span = pl.ds(c * CHUNK, CHUNK)
+            v_ref[:, span] = v_ref[:, span] - w_ref[:, span] * eb_ref[:, span]
         slab_part(2)
         for j in range(1, first):
             first_arrival(j).wait_recv()

time: 28.5 us -> 27.2 us (0.954)
  Pallas kernels: 27.7 us -> 26.4 us
    pallas_call x1, Pallas kernels: 26.7 us -> 25.3 us  [on_device(): call(fields, wet_land, links, surface_diagonal, spread, mixing, thickness)]
where the time goes in v3:
time: 27.2 us; the launch traced here: 27.1 us
  Pallas kernels  26.4 us (97%)
  between operations  0.64 us (2%)
    pallas_call x1, Pallas kernels, on_device(): call(fields, wet_land, links, surface_diagonal, spread, mixing, thickness)  25.3 us
    pallas_call x1, Pallas kernels, put(): pl.pallas_call(kernel, out_shape=tuple((jax.ShapeDtypeStruct(x.shape, x.d...  1.09 us

profile of v3, /device:TPU:0, one launch (start us, length us, event | category | flops | bytes accessed | tf_op | source)
XLA Modules:
  0.0 27.1 jit_solution(6061612623527964823)
XLA Ops:
  0.6 25.3 %shard_map.94 = (f32[1,1,3,3,4,8100]{5,4,3,2,1,0:T(4,128)S(1)}, f32[1,3,1,8100]{3,2,1,0:T(1,128)S(1)}, f32[1,3,1,8100]{3,2,1,0:T(1,128)S(1)}) custom-call(f32[1,1,3,3,4,8100]{5,4,3,2,1,0:T(4,128)} %fields.1, s32[1,3,1,8100]{3,2,1,0:T(1,128)} %bitcast.8, s32[1,1,3,4,4]{4,3,2,1,0:T(4,128)} %links_in.1, f32[1,3,1,8100]{3,2,1,0:T(1,128)} %bitcast.9, ...), custom_call_target="tpu_custom_call" | custom-call | tf_op jit(solution)/shard_map/pallas_call | solution.py:648
  26.0 1.1 %shard_map.95 = (f32[1,1,3,3,4,8100]{5,4,3,2,1,0:T(4,128)}, f32[1,3,1,8100]{3,2,1,0:T(1,128)}, f32[1,3,1,8100]{3,2,1,0:T(1,128)}) custom-call(f32[1,1,3,3,4,8100]{5,4,3,2,1,0:T(4,128)S(1)} %get-tuple-element.9.refs_0_, f32[1,3,1,8100]{3,2,1,0:T(1,128)S(1)} %get-tuple-element.10.refs_1_, f32[1,3,1,8100]{3,2,1,0:T(1,128)S(1)} %get-tuple-element.11.refs_2_), custom_call_target="tpu_custom_call" | custom-call | tf_op jit(solution)/shard_map/pallas_call | solution.py:631
